TPU v7x, 32 devices: a whole 2x2x4 slice. The times are simulated.
32 devices in a mesh: row: 8 (over z, y), basis: 4 (over x, core).
Axes of the slice: x: 2, y: 2, z: 4, core: 2. Of those that a mesh axis runs over, the one named last changes fastest.
Arguments:
- design: float32 [7680, 40960], P('row', 'basis'), may hold values from -0.029646354 to 0.029646354
- targets: float32 [7680], P('row'), may hold values from -6 to 6
- counts: int32 [7680, 128], P('row'), may hold values from 0 to 3
- coefficients: float32 [40960, 128], P('basis'), may hold values from -6 to 6
- step_size: float32 [128], replicated, may hold values from 0.03 to 0.15
Outputs:
- fitted: float32 [40960, 128], P('basis')
- influence: float32 [7680, 128], P('row')
All inputs are finite; a program needn't handle non-finite values.
Results may differ from a plain program's by a relative error of at most 0.00017.
Values sent between devices are 32-bit elements; how exact they have to be, the bound alone decides.
No kernel may reach another device: no remote copies, remote signals or barrier semaphores. Data moves between devices by JAX's collectives and lax.ppermute only.
A program may use at most 128 MiB of HBM per device.

v0:
```python
import jax
import jax.numpy as jnp
from jax import lax
from jax.sharding import PartitionSpec as P

STEPS = 3
HIGH = lax.Precision.HIGHEST


def transposed(left, right):
    return lax.dot_general(
        left, right, (((0,), (0,)), ((), ())), precision=HIGH, preferred_element_type=jnp.float32
    )


def predictions(partial_value):
    return lax.psum(partial_value, "basis")


def weighted(predicted, targets, weights):
    residual = predicted - targets[:, None]
    return weights * residual / jnp.sqrt(1.0 + residual * residual)


def shards(design, targets, counts, coefficients, step_size):
    weights = counts.astype(jnp.float32)
    curve_term = transposed(design * design, weights)
    influence = jnp.zeros((design.shape[0], coefficients.shape[1]), jnp.float32)
    share_rows = coefficients.shape[0] // lax.axis_size("row")
    offset = lax.axis_index("row") * share_rows
    curvature = lax.psum_scatter(curve_term, "row", scatter_dimension=0, tiled=True) + 0.01
    share = lax.dynamic_slice_in_dim(coefficients, offset, share_rows, 0)
    for step in range(STEPS):
        if step == 0:
            partial_value = jnp.dot(
                design, coefficients, precision=HIGH, preferred_element_type=jnp.float32
            )
        else:
            partial_value = jnp.dot(
                design,
                lax.all_gather(share, "row", axis=0, tiled=True),
                precision=HIGH,
                preferred_element_type=jnp.float32,
            )
        influence = weighted(predictions(partial_value), targets, weights)
        gradient = lax.psum_scatter(
            transposed(design, influence), "row", scatter_dimension=0, tiled=True
        )
        share = share - step_size[None, :] * gradient / curvature
    fitted = lax.all_gather(share, "row", axis=0, tiled=True)
    return (fitted, influence)


def solution(mesh):
    return jax.shard_map(
        shards,
        mesh=mesh,
        in_specs=(P("row", "basis"), P("row"), P("row", None), P("basis", None), P()),
        out_specs=(P("basis", None), P("row", None)),
        check_vma=False,
    )
```

profile of v0, /device:TPU:0, one launch (start us, length us, event | category | flops | bytes accessed | tf_op | source)
XLA Modules:
  0.0 961.2 jit_solution(473307508805316564)
XLA Ops:
  8.1 35.6 %fusion.23 = f32[960,128]{1,0:T(8,128)} fusion(f32[960,10240]{1,0:T(8,128)} %param.5, f32[10240,128]{1,0:T(8,128)} %param.8), kind=kOutput, calls=%fused_computation.33 | convolution fusion | flops 15099494400 | bytes 45056000 | tf_op jit(solution)/shard_map/dot_general | solution.py:35
  43.6 0.0 reduce-scatter.7.cloned.1.call-start
  43.7 29.3 %fusion = f32[10240,128]{0,1:T(8,128)} fusion(f32[960,10240]{1,0:T(8,128)} %param.5, s32[960,128]{1,0:T(8,128)S(1)} %copy-done), kind=kOutput, calls=%fused_computation | convolution fusion | flops 15109447680 | bytes 45056000 | tf_op jit(solution)/shard_map/dot_general | solution.py:11
  73.1 0.6 reduce-scatter.5.cloned.1.call-start
  73.6 6.2 all-reduce.4.cloned.1.call-done
  79.8 29.3 %convolution_bitcast_fusion.2 = f32[10240,128]{0,1:T(8,128)} fusion(f32[960,10240]{1,0:T(8,128)} %param.5, f32[960,128]{1,0:T(8,128)} %all-reduce.4.cloned.1.call-done, s32[960,128]{1,0:T(8,128)S(1)} %copy-done, f32[960]{0:T(1024)S(1)} %copy-done.5), kind=kOutput, calls=%fused_computation.4 | convolution fusion | flops 15100231680 | bytes 45551360 | tf_op jit(solution)/shard_map/dot_general | solution.py:11
  109.1 0.0 all-gather.4.cloned.1.call-start
  109.2 1.1 constant_dynamic-slice_fusion
  110.3 0.2 copy.11
  110.6 68.3 %reduce-scatter.7.cloned.1.call-done = f32[1280,128]{0,1:T(8,128)} async-done(((f32[10240,128]{0,1:T(8,128)}), f32[1280,128]{0,1:T(8,128)}) %reduce-scatter.7.cloned.1.call-update) | async-done | bytes 655376 | tf_op jit(solution)/shard_map/reduce_scatter | solution.py:31
  178.9 106.6 %reduce-scatter.5.cloned.1.call-done = f32[1280,128]{0,1:T(8,128)} async-done(((f32[10240,128]{0,1:T(8,128)}), f32[1280,128]{0,1:T(8,128)}) %reduce-scatter.5.cloned.1.call-update) | async-done | bytes 655376 | tf_op jit(solution)/shard_map/reduce_scatter | solution.py:46
  285.5 2.3 divide_subtract_fusion.2
  287.8 0.2 all-reduce.6.cloned.1.call-start
  288.0 85.1 %all-gather.4.cloned.1.call-done = f32[10240,128]{0,1:T(8,128)} async-done(((f32[1280,128]{0,1:T(8,128)}), f32[10240,128]{0,1:T(8,128)}) %all-gather.4.cloned.1.call-update) | async-done | bytes 5242896 | tf_op jit(solution)/shard_map/all_gather | solution.py:41
  373.2 35.7 %convolution_bitcast_fusion.4 = f32[960,128]{1,0:T(8,128)} fusion(f32[10240,128]{0,1:T(8,128)} %all-gather.4.cloned.1.call-done, f32[960,10240]{1,0:T(8,128)} %param.5), kind=kOutput, calls=%fused_computation.6 | convolution fusion | flops 15099494400 | bytes 45056000 | tf_op jit(solution)/shard_map/dot_general | solution.py:39
  408.8 0.3 reduce-scatter.9.cloned.1.call-start
  409.1 31.5 %all-reduce.6.cloned.1.call-done = f32[960,128]{1,0:T(8,128)} async-done(((f32[960,128]{1,0:T(8,128)}), f32[960,128]{1,0:T(8,128)}) %all-reduce.6.cloned.1.call-update) | async-done | bytes 491536 | tf_op jit(solution)/shard_map/psum | solution.py:17
  440.6 29.0 %convolution_bitcast_fusion.1 = f32[10240,128]{0,1:T(8,128)} fusion(f32[960,10240]{1,0:T(8,128)} %param.5, f32[960,128]{1,0:T(8,128)} %all-reduce.6.cloned.1.call-done, s32[960,128]{1,0:T(8,128)S(1)} %copy-done, f32[960]{0:T(1024)S(1)} %copy-done.5), kind=kOutput, calls=%fused_computation.3 | convolution fusion | flops 15100231680 | bytes 45551360 | tf_op jit(solution)/shard_map/dot_general | solution.py:11
  469.6 103.1 %reduce-scatter.9.cloned.1.call-done = f32[1280,128]{0,1:T(8,128)} async-done(((f32[10240,128]{0,1:T(8,128)}), f32[1280,128]{0,1:T(8,128)}) %reduce-scatter.9.cloned.1.call-update) | async-done | bytes 655376 | tf_op jit(solution)/shard_map/reduce_scatter | solution.py:46
  572.7 2.1 divide_subtract_fusion.1
  574.9 0.3 all-reduce.8.cloned.1.call-start
  575.2 85.0 %all-gather.6.cloned.1.call-done = f32[10240,128]{0,1:T(8,128)} async-done(((f32[1280,128]{0,1:T(8,128)}), f32[10240,128]{0,1:T(8,128)}) %all-gather.6.cloned.1.call-update) | async-done | bytes 5242896 | tf_op jit(solution)/shard_map/all_gather | solution.py:41
  660.2 35.7 %convolution_bitcast_fusion.3 = f32[960,128]{1,0:T(8,128)} fusion(f32[10240,128]{0,1:T(8,128)} %all-gather.6.cloned.1.call-done, f32[960,10240]{1,0:T(8,128)} %param.5), kind=kOutput, calls=%fused_computation.5 | convolution fusion | flops 15099494400 | bytes 45056000 | tf_op jit(solution)/shard_map/dot_general | solution.py:39
  695.9 0.3 reduce-scatter.11.cloned.1.call-start
  696.2 31.4 %all-reduce.8.cloned.1.call-done = f32[960,128]{1,0:T(8,128)} async-done(((f32[960,128]{1,0:T(8,128)}), f32[960,128]{1,0:T(8,128)}) %all-reduce.8.cloned.1.call-update) | async-done | bytes 491536 | tf_op jit(solution)/shard_map/psum | solution.py:17
  727.6 1.2 rsqrt_multiply_fusion
  728.9 27.8 %convolution_bitcast_fusion = f32[10240,128]{0,1:T(8,128)} fusion(f32[960,128]{1,0:T(8,128)S(1)} %rsqrt_multiply_fusion, f32[960,10240]{1,0:T(8,128)} %param.5), kind=kOutput, calls=%fused_computation.2 | convolution fusion | flops 15099494400 | bytes 45056000 | tf_op jit(solution)/shard_map/dot_general | solution.py:11
  756.7 0.0 all-gather.8.cloned.1.call-start
  756.8 103.1 %reduce-scatter.11.cloned.1.call-done = f32[1280,128]{0,1:T(8,128)} async-done(((f32[10240,128]{0,1:T(8,128)}), f32[1280,128]{0,1:T(8,128)}) %reduce-scatter.11.cloned.1.call-update) | async-done | bytes 655376 | tf_op jit(solution)/shard_map/reduce_scatter | solution.py:46
  859.8 2.1 divide_subtract_fusion
  861.9 85.8 %all-gather.8.cloned.1.call-done = f32[10240,128]{0,1:T(8,128)} async-done(((f32[1280,128]{0,1:T(8,128)}), f32[10240,128]{0,1:T(8,128)}) %all-gather.8.cloned.1.call-update) | async-done | bytes 5242896 | tf_op jit(solution)/shard_map/all_gather | solution.py:50
  947.7 5.9 copy.9
  (26 shorter events, 0.3 us)
Async XLA Ops:
  8.0 35.7 %copy-start = (s32[960,128]{1,0:T(8,128)S(1)}, s32[960,128]{1,0:T(8,128)}, u32[]{:S(2)}) copy-start(s32[960,128]{1,0:T(8,128)} %param.7) | copy-start | bytes 1474564
  8.0 71.8 %all-reduce.4.cloned.1.call-start = ((), (), s32[]{:S(2)}) async-start(), calls=%async_computation.4 | async-start | bytes 983040 | tf_op jit(solution)/shard_map/psum | solution.py:17
  43.6 36.2 %copy-start.5 = (f32[960]{0:T(1024)S(1)}, f32[960]{0:T(1024)}, u32[]{:S(2)}) copy-start(f32[960]{0:T(1024)} %param.6) | copy-start | bytes 11524
  43.6 135.2 %reduce-scatter.7.cloned.1.call-start = ((), (), s32[]{:S(2)}) async-start(), calls=%async_computation.6 | async-start | bytes 5898240 | tf_op jit(solution)/shard_map/reduce_scatter | solution.py:31
  73.1 212.4 %copy-start.6 = (f32[128]{0:T(128)S(1)}, f32[128]{0:T(128)}, u32[]{:S(2)}) copy-start(f32[128]{0:T(128)} %param.9) | copy-start | bytes 1540
  73.1 212.4 %reduce-scatter.5.cloned.1.call-start = ((), (), s32[]{:S(2)}) async-start(), calls=%async_computation.5 | async-start | bytes 5898240 | tf_op jit(solution)/shard_map/reduce_scatter | solution.py:46
  109.1 264.0 %all-gather.4.cloned.1.call-start = ((), (), s32[]{:S(2)}) async-start(), calls=%async_computation.7 | async-start | bytes 5898240 | tf_op jit(solution)/shard_map/all_gather | solution.py:41
  287.8 152.8 %all-reduce.6.cloned.1.call-start = ((), (), s32[]{:S(2)}) async-start(), calls=%async_computation.8 | async-start | bytes 983040 | tf_op jit(solution)/shard_map/psum | solution.py:17
  408.8 163.9 %copy-start.2 = (f32[1280,128]{0,1:T(8,128)S(1)}, f32[1280,128]{0,1:T(8,128)}, u32[]{:S(2)}) copy-start(f32[1280,128]{0,1:T(8,128)} %divide_subtract_fusion.2) | copy-start | bytes 1966084
  408.8 163.9 %copy-start.3 = (f32[1280,128]{0,1:T(8,128)S(1)}, f32[1280,128]{0,1:T(8,128)}, u32[]{:S(2)}) copy-start(f32[1280,128]{0,1:T(8,128)} %reduce-scatter.7.cloned.1.call-done) | copy-start | bytes 1966084
  408.8 163.9 %reduce-scatter.9.cloned.1.call-start = ((), (), s32[]{:S(2)}) async-start(), calls=%async_computation.9 | async-start | bytes 5898240 | tf_op jit(solution)/shard_map/reduce_scatter | solution.py:46
  469.6 190.6 %all-gather.6.cloned.1.call-start = ((), (), s32[]{:S(2)}) async-start(), calls=%async_computation.10 | async-start | bytes 5898240 | tf_op jit(solution)/shard_map/all_gather | solution.py:41
  574.9 152.8 %all-reduce.8.cloned.1.call-start = ((), (), s32[]{:S(2)}) async-start(), calls=%async_computation.11 | async-start | bytes 983040 | tf_op jit(solution)/shard_map/psum | solution.py:17
  695.8 164.0 %copy-start.1 = (f32[1280,128]{0,1:T(8,128)S(1)}, f32[1280,128]{0,1:T(8,128)}, u32[]{:S(2)}) copy-start(f32[1280,128]{0,1:T(8,128)} %divide_subtract_fusion.1) | copy-start | bytes 1966084
  695.9 163.9 %reduce-scatter.11.cloned.1.call-start = ((), (), s32[]{:S(2)}) async-start(), calls=%async_computation.12 | async-start | bytes 5898240 | tf_op jit(solution)/shard_map/reduce_scatter | solution.py:46
  728.8 224.7 %copy-start.4 = (f32[960,128]{1,0:T(8,128)}, f32[960,128]{1,0:T(8,128)S(1)}, u32[]{:S(2)}) copy-start(f32[960,128]{1,0:T(8,128)S(1)} %rsqrt_multiply_fusion) | copy-start | bytes 1474564
  756.7 191.0 %all-gather.8.cloned.1.call-start = ((), (), s32[]{:S(2)}) async-start(), calls=%async_computation.13 | async-start | bytes 5898240 | tf_op jit(solution)/shard_map/all_gather | solution.py:50
Sparse Core Ops, SparseCore 0:
  43.8 36.0 all-reduce.3
  409.0 31.5 all-reduce.5
  696.0 31.5 all-reduce.7
Sparse Core Ops, SparseCore 1:
  73.1 105.7 reduce-scatter.6
  182.9 102.5 reduce-scatter.4
  287.9 85.2 all-gather.3
  469.7 103.0 reduce-scatter.8
  574.9 85.2 all-gather.5
  756.8 103.0 reduce-scatter.10
  862.5 85.2 all-gather.7
where the time goes:
time: 969 us; the launch traced here: 961 us
  waiting for transfers between devices  706 us (73%)
  matrix products  222 us (23%)
  between operations  15.9 us (2%)
    reduce_scatter x3, waiting for transfers between devices, shards(): lax.psum_scatter(transposed(design, influence), 'row', scatter_dimension=...  313 us
    all_gather x2, waiting for transfers between devices, shards(): lax.all_gather(share, 'row', axis=0, tiled=True)  170 us
    dot_general x4, matrix products, transposed(): lax.dot_general(left, right, (((0,), (0,)), ((), ())), precision=HIGH, pr...  115 us
    all_gather x1, waiting for transfers between devices, shards(): fitted = lax.all_gather(share, 'row', axis=0, tiled=True)  85.8 us
    dot_general x2, matrix products, shards(): jnp.dot(design, lax.all_gather(share, 'row', axis=0, tiled=True), precisi...  71.3 us
    psum x3, waiting for transfers between devices, predictions(): return lax.psum(partial_value, 'basis')  69 us
    reduce_scatter x1, waiting for transfers between devices, shards(): lax.psum_scatter(curve_term, 'row', scatter_dimension=0, tiled=True) + 0.01  68.3 us
    dot_general x1, matrix products, shards(): jnp.dot(design, coefficients, precision=HIGH, preferred_element_type=jnp....  35.6 us
  transfers between devices with their start and end apart: 10, of which 10 were waited for; matrix products, arithmetic and copies ran while one was open for 6% of the time, Pallas kernels for 0%

commit v1 on v0

--- a/solution.py
+++ b/solution.py
@@ -47,7 +47,12 @@
             transposed(design, influence), "row", scatter_dimension=0, tiled=True
         )
         share = share - step_size[None, :] * gradient / curvature
-    fitted = lax.all_gather(share, "row", axis=0, tiled=True)
+    ring = [share]
+    for hop in range(7):
+        ring.append(lax.ppermute(ring[-1], "row", [(dev, (dev + 1) % 8) for dev in range(8)]))
+    fitted = jnp.roll(
+        jnp.concatenate(ring[::-1], axis=0), (lax.axis_index("row") + 1) * ring[0].shape[0], axis=0
+    )
     return (fitted, influence)
 
 

time: 969 us -> 1010 us (1.042)
  waiting for transfers between devices: 706 us -> 733 us
  local copies, waits for them, and re-layouts: 7.27 us -> 20.3 us
    ppermute x0 -> x7, waiting for transfers between devices: none -> 112 us  [shards(): lax.ppermute(ring[-1], 'row', [(dev, (dev + 1) % 8) for dev in range(8)])]
    all_gather x1 -> x0, waiting for transfers between devices: 85.8 us -> none  [shards(): fitted = lax.all_gather(share, 'row', axis=0, tiled=True)]
  transfers between devices with their start and end apart: 10 -> 16, of which waited for: 10 -> 16; matrix products, arithmetic and copies ran while one was open for 6% -> 6% of each run, Pallas kernels for 0% -> 0%
where the time goes in v1:
time: 1010 us; the launch traced here: 1000 us
  waiting for transfers between devices  733 us (73%)
  matrix products  222 us (22%)
  local copies, waits for them, and re-layouts  20.3 us (2%)
  between operations  15.7 us (2%)
    reduce_scatter x3, waiting for transfers between devices, shards(): lax.psum_scatter(transposed(design, influence), 'row', scatter_dimension=...  313 us
    all_gather x2, waiting for transfers between devices, shards(): lax.all_gather(share, 'row', axis=0, tiled=True)  170 us
    dot_general x4, matrix products, transposed(): lax.dot_general(left, right, (((0,), (0,)), ((), ())), precision=HIGH, pr...  115 us
    ppermute x7, waiting for transfers between devices, shards(): lax.ppermute(ring[-1], 'row', [(dev, (dev + 1) % 8) for dev in range(8)])  112 us
    dot_general x2, matrix products, shards(): jnp.dot(design, lax.all_gather(share, 'row', axis=0, tiled=True), precisi...  71.3 us
    psum x3, waiting for transfers between devices, predictions(): return lax.psum(partial_value, 'basis')  69.6 us
    reduce_scatter x1, waiting for transfers between devices, shards(): lax.psum_scatter(curve_term, 'row', scatter_dimension=0, tiled=True) + 0.01  68.2 us
    dot_general x1, matrix products, shards(): jnp.dot(design, coefficients, precision=HIGH, preferred_element_type=jnp....  35.6 us
  transfers between devices with their start and end apart: 16, of which 16 were waited for; matrix products, arithmetic and copies ran while one was open for 6% of the time, Pallas kernels for 0%

profile of v1, /device:TPU:0, one launch (start us, length us, event | category | flops | bytes accessed | tf_op | source)
XLA Modules:
  0.0 1001.1 jit_solution(9278459644424200290)
XLA Ops:
  8.1 35.6 %fusion.23 = f32[960,128]{1,0:T(8,128)} fusion(f32[960,10240]{1,0:T(8,128)} %param.5, f32[10240,128]{1,0:T(8,128)} %param.8), kind=kOutput, calls=%fused_computation.50 | convolution fusion | flops 15099494400 | bytes 45056000 | tf_op jit(solution)/shard_map/dot_general | solution.py:35
  43.7 29.3 %fusion = f32[10240,128]{0,1:T(8,128)} fusion(f32[960,10240]{1,0:T(8,128)} %param.5, s32[960,128]{1,0:T(8,128)S(1)} %copy-done), kind=kOutput, calls=%fused_computation | convolution fusion | flops 15109447680 | bytes 45056000 | tf_op jit(solution)/shard_map/dot_general | solution.py:11
  73.3 6.6 all-reduce.4.cloned.1.call-done
  79.9 29.3 %convolution_bitcast_fusion.2 = f32[10240,128]{0,1:T(8,128)} fusion(f32[960,10240]{1,0:T(8,128)} %param.5, f32[960,128]{1,0:T(8,128)} %all-reduce.4.cloned.1.call-done, s32[960,128]{1,0:T(8,128)S(1)} %copy-done, f32[960]{0:T(1024)S(1)} %copy-done.9), kind=kOutput, calls=%fused_computation.4 | convolution fusion | flops 15100231680 | bytes 45551360 | tf_op jit(solution)/shard_map/dot_general | solution.py:11
  110.6 68.2 %reduce-scatter.7.cloned.1.call-done = f32[1280,128]{0,1:T(8,128)} async-done(((f32[10240,128]{0,1:T(8,128)}), f32[1280,128]{0,1:T(8,128)}) %reduce-scatter.7.cloned.1.call-update) | async-done | bytes 655376 | tf_op jit(solution)/shard_map/reduce_scatter | solution.py:31
  178.8 106.6 %reduce-scatter.5.cloned.1.call-done = f32[1280,128]{0,1:T(8,128)} async-done(((f32[10240,128]{0,1:T(8,128)}), f32[1280,128]{0,1:T(8,128)}) %reduce-scatter.5.cloned.1.call-update) | async-done | bytes 655376 | tf_op jit(solution)/shard_map/reduce_scatter | solution.py:46
  285.4 2.3 divide_subtract_fusion.2
  288.0 85.1 %all-gather.3.cloned.1.call-done = f32[10240,128]{0,1:T(8,128)} async-done(((f32[1280,128]{0,1:T(8,128)}), f32[10240,128]{0,1:T(8,128)}) %all-gather.3.cloned.1.call-update) | async-done | bytes 5242896 | tf_op jit(solution)/shard_map/all_gather | solution.py:41
  373.1 35.6 %convolution_bitcast_fusion.4 = f32[960,128]{1,0:T(8,128)} fusion(f32[10240,128]{0,1:T(8,128)} %all-gather.3.cloned.1.call-done, f32[960,10240]{1,0:T(8,128)} %param.5), kind=kOutput, calls=%fused_computation.6 | convolution fusion | flops 15099494400 | bytes 45056000 | tf_op jit(solution)/shard_map/dot_general | solution.py:39
  409.1 31.4 %all-reduce.6.cloned.1.call-done = f32[960,128]{1,0:T(8,128)} async-done(((f32[960,128]{1,0:T(8,128)}), f32[960,128]{1,0:T(8,128)}) %all-reduce.6.cloned.1.call-update) | async-done | bytes 491536 | tf_op jit(solution)/shard_map/psum | solution.py:17
  440.6 29.0 %convolution_bitcast_fusion.1 = f32[10240,128]{0,1:T(8,128)} fusion(f32[960,10240]{1,0:T(8,128)} %param.5, f32[960,128]{1,0:T(8,128)} %all-reduce.6.cloned.1.call-done, s32[960,128]{1,0:T(8,128)S(1)} %copy-done, f32[960]{0:T(1024)S(1)} %copy-done.9), kind=kOutput, calls=%fused_computation.3 | convolution fusion | flops 15100231680 | bytes 45551360 | tf_op jit(solution)/shard_map/dot_general | solution.py:11
  469.6 103.1 %reduce-scatter.9.cloned.1.call-done = f32[1280,128]{0,1:T(8,128)} async-done(((f32[10240,128]{0,1:T(8,128)}), f32[1280,128]{0,1:T(8,128)}) %reduce-scatter.9.cloned.1.call-update) | async-done | bytes 655376 | tf_op jit(solution)/shard_map/reduce_scatter | solution.py:46
  572.7 2.1 divide_subtract_fusion.1
  575.4 84.8 %all-gather.5.cloned.1.call-done = f32[10240,128]{0,1:T(8,128)} async-done(((f32[1280,128]{0,1:T(8,128)}), f32[10240,128]{0,1:T(8,128)}) %all-gather.5.cloned.1.call-update) | async-done | bytes 5242896 | tf_op jit(solution)/shard_map/all_gather | solution.py:41
  660.2 35.6 %convolution_bitcast_fusion.3 = f32[960,128]{1,0:T(8,128)} fusion(f32[10240,128]{0,1:T(8,128)} %all-gather.5.cloned.1.call-done, f32[960,10240]{1,0:T(8,128)} %param.5), kind=kOutput, calls=%fused_computation.5 | convolution fusion | flops 15099494400 | bytes 45056000 | tf_op jit(solution)/shard_map/dot_general | solution.py:39
  696.1 31.5 %all-reduce.8.cloned.1.call-done = f32[960,128]{1,0:T(8,128)} async-done(((f32[960,128]{1,0:T(8,128)}), f32[960,128]{1,0:T(8,128)}) %all-reduce.8.cloned.1.call-update) | async-done | bytes 491536 | tf_op jit(solution)/shard_map/psum | solution.py:17
  727.6 1.2 rsqrt_multiply_fusion
  728.9 27.9 %convolution_bitcast_fusion = f32[10240,128]{0,1:T(8,128)} fusion(f32[960,128]{1,0:T(8,128)S(1)} %rsqrt_multiply_fusion, f32[960,10240]{1,0:T(8,128)} %param.5), kind=kOutput, calls=%fused_computation.2 | convolution fusion | flops 15099494400 | bytes 45056000 | tf_op jit(solution)/shard_map/dot_general | solution.py:11
  756.8 103.1 %reduce-scatter.11.cloned.1.call-done = f32[1280,128]{0,1:T(8,128)} async-done(((f32[10240,128]{0,1:T(8,128)}), f32[1280,128]{0,1:T(8,128)}) %reduce-scatter.11.cloned.1.call-update) | async-done | bytes 655376 | tf_op jit(solution)/shard_map/reduce_scatter | solution.py:46
  859.9 1.3 divide_subtract_fusion
  861.2 1.5 collective-permute-start
  862.7 17.2 %collective-permute-done = f32[1280,128]{0,1:T(8,128)S(1)} collective-permute-done((f32[1280,128]{0,1:T(8,128)S(1)}, f32[1280,128]{0,1:T(8,128)S(1)}, u32[]{:S(2)}, u32[]{:S(2)}) %collective-permute-start) | collective-permute-done | bytes 655392 | tf_op jit(solution)/shard_map/ppermute | solution.py:52
  879.9 17.9 %collective-permute-done.1 = f32[1280,128]{0,1:T(8,128)S(1)} collective-permute-done((f32[1280,128]{0,1:T(8,128)S(1)}, f32[1280,128]{0,1:T(8,128)S(1)}, u32[]{:S(2)}, u32[]{:S(2)}) %collective-permute-start.1) | collective-permute-done | bytes 655392 | tf_op jit(solution)/shard_map/ppermute | solution.py:52
  897.8 17.0 %collective-permute-done.2 = f32[1280,128]{0,1:T(8,128)S(1)} collective-permute-done((f32[1280,128]{0,1:T(8,128)S(1)}, f32[1280,128]{0,1:T(8,128)S(1)}, u32[]{:S(2)}, u32[]{:S(2)}) %collective-permute-start.2) | collective-permute-done | bytes 655392 | tf_op jit(solution)/shard_map/ppermute | solution.py:52
  914.8 16.1 %collective-permute-done.3 = f32[1280,128]{0,1:T(8,128)S(1)} collective-permute-done((f32[1280,128]{0,1:T(8,128)S(1)}, f32[1280,128]{0,1:T(8,128)S(1)}, u32[]{:S(2)}, u32[]{:S(2)}) %collective-permute-start.3) | collective-permute-done | bytes 655392 | tf_op jit(solution)/shard_map/ppermute | solution.py:52
  931.8 15.3 %collective-permute-done.4 = f32[1280,128]{0,1:T(8,128)S(1)} collective-permute-done((f32[1280,128]{0,1:T(8,128)S(1)}, f32[1280,128]{0,1:T(8,128)S(1)}, u32[]{:S(2)}, u32[]{:S(2)}) %collective-permute-start.4) | collective-permute-done | bytes 655392 | tf_op jit(solution)/shard_map/ppermute | solution.py:52
  947.9 14.7 %collective-permute-done.5 = f32[1280,128]{0,1:T(8,128)} collective-permute-done((f32[1280,128]{0,1:T(8,128)S(1)}, f32[1280,128]{0,1:T(8,128)}, u32[]{:S(2)}, u32[]{:S(2)}) %collective-permute-start.5) | collective-permute-done | bytes 655392 | tf_op jit(solution)/shard_map/ppermute | solution.py:52
  962.6 13.9 %collective-permute-done.6 = f32[1280,128]{0,1:T(8,128)} collective-permute-done((f32[1280,128]{0,1:T(8,128)}, f32[1280,128]{0,1:T(8,128)}, u32[]{:S(2)}, u32[]{:S(2)}) %collective-permute-start.6) | collective-permute-done | bytes 655392 | tf_op jit(solution)/shard_map/ppermute | solution.py:52
  977.6 1.1 constant_dynamic-update-slice_fusion.14
  978.8 1.1 constant_dynamic-update-slice_fusion.13
  984.1 3.8 constant_dynamic-slice_fusion
  987.9 5.9 copy.9
  (62 shorter events, 10.1 us)
Async XLA Ops:
  8.0 35.7 %copy-start = (s32[960,128]{1,0:T(8,128)S(1)}, s32[960,128]{1,0:T(8,128)}, u32[]{:S(2)}) copy-start(s32[960,128]{1,0:T(8,128)} %param.7) | copy-start | bytes 1474564
  8.0 71.9 %all-reduce.4.cloned.1.call-start = ((), (), s32[]{:S(2)}) async-start(), calls=%async_computation.4 | async-start | bytes 983040 | tf_op jit(solution)/shard_map/psum | solution.py:17
  43.6 36.2 %copy-start.9 = (f32[960]{0:T(1024)S(1)}, f32[960]{0:T(1024)}, u32[]{:S(2)}) copy-start(f32[960]{0:T(1024)} %param.6) | copy-start | bytes 11524
  43.6 135.2 %reduce-scatter.7.cloned.1.call-start = ((), (), s32[]{:S(2)}) async-start(), calls=%async_computation.6 | async-start | bytes 5898240 | tf_op jit(solution)/shard_map/reduce_scatter | solution.py:31
  73.1 212.4 %copy-start.10 = (f32[128]{0:T(128)S(1)}, f32[128]{0:T(128)}, u32[]{:S(2)}) copy-start(f32[128]{0:T(128)} %param.9) | copy-start | bytes 1540
  73.1 212.4 %reduce-scatter.5.cloned.1.call-start = ((), (), s32[]{:S(2)}) async-start(), calls=%async_computation.5 | async-start | bytes 5898240 | tf_op jit(solution)/shard_map/reduce_scatter | solution.py:46
  109.2 263.9 %all-gather.3.cloned.1.call-start = ((), (), s32[]{:S(2)}) async-start(), calls=%async_computation.7 | async-start | bytes 5898240 | tf_op jit(solution)/shard_map/all_gather | solution.py:41
  287.8 152.8 %all-reduce.6.cloned.1.call-start = ((), (), s32[]{:S(2)}) async-start(), calls=%async_computation.8 | async-start | bytes 983040 | tf_op jit(solution)/shard_map/psum | solution.py:17
  408.8 163.9 %copy-start.1 = (f32[1280,128]{0,1:T(8,128)S(1)}, f32[1280,128]{0,1:T(8,128)}, u32[]{:S(2)}) copy-start(f32[1280,128]{0,1:T(8,128)} %divide_subtract_fusion.2) | copy-start | bytes 1966084
  408.8 163.9 %copy-start.3 = (f32[1280,128]{0,1:T(8,128)S(1)}, f32[1280,128]{0,1:T(8,128)}, u32[]{:S(2)}) copy-start(f32[1280,128]{0,1:T(8,128)} %reduce-scatter.7.cloned.1.call-done) | copy-start | bytes 1966084
  408.8 163.9 %reduce-scatter.9.cloned.1.call-start = ((), (), s32[]{:S(2)}) async-start(), calls=%async_computation.9 | async-start | bytes 5898240 | tf_op jit(solution)/shard_map/reduce_scatter | solution.py:46
  469.6 190.6 %all-gather.5.cloned.1.call-start = ((), (), s32[]{:S(2)}) async-start(), calls=%async_computation.10 | async-start | bytes 5898240 | tf_op jit(solution)/shard_map/all_gather | solution.py:41
  574.8 152.8 %all-reduce.8.cloned.1.call-start = ((), (), s32[]{:S(2)}) async-start(), calls=%async_computation.11 | async-start | bytes 983040 | tf_op jit(solution)/shard_map/psum | solution.py:17
  695.9 164.0 %reduce-scatter.11.cloned.1.call-start = ((), (), s32[]{:S(2)}) async-start(), calls=%async_computation.12 | async-start | bytes 5898240 | tf_op jit(solution)/shard_map/reduce_scatter | solution.py:46
  728.9 27.9 %copy-start.4 = (f32[960,128]{1,0:T(8,128)}, f32[960,128]{1,0:T(8,128)S(1)}, u32[]{:S(2)}) copy-start(f32[960,128]{1,0:T(8,128)S(1)} %rsqrt_multiply_fusion) | copy-start | bytes 1474564
  728.9 131.0 %copy-start.2 = (f32[1280,128]{0,1:T(8,128)S(1)}, f32[1280,128]{0,1:T(8,128)}, u32[]{:S(2)}) copy-start(f32[1280,128]{0,1:T(8,128)} %divide_subtract_fusion.1) | copy-start | bytes 1966084
  861.2 18.8 %collective-permute-start = (f32[1280,128]{0,1:T(8,128)S(1)}, f32[1280,128]{0,1:T(8,128)S(1)}, u32[]{:S(2)}, u32[]{:S(2)}) collective-permute-start(f32[1280,128]{0,1:T(8,128)S(1)} %divide_subtract_fusion), channel_id=1, source_target_pairs={{0,4},{4,8},{8,12},{12,16},{16,20},{20,24},{24,28},{28,0},{1,5},{5... | collective-permute-start | bytes 1966088 | tf_op jit(solution)/shard_map/ppermute | solution.py:52
  879.9 17.9 %collective-permute-start.1 = (f32[1280,128]{0,1:T(8,128)S(1)}, f32[1280,128]{0,1:T(8,128)S(1)}, u32[]{:S(2)}, u32[]{:S(2)}) collective-permute-start(f32[1280,128]{0,1:T(8,128)S(1)} %collective-permute-done), channel_id=1, source_target_pairs={{0,4},{4,8},{8,12},{12,16},{16,20},{20,24},{24,28},{28,0},{1,5},{5... | collective-permute-start | bytes 1966088 | tf_op jit(solution)/shard_map/ppermute | solution.py:52
  897.8 17.0 %collective-permute-start.2 = (f32[1280,128]{0,1:T(8,128)S(1)}, f32[1280,128]{0,1:T(8,128)S(1)}, u32[]{:S(2)}, u32[]{:S(2)}) collective-permute-start(f32[1280,128]{0,1:T(8,128)S(1)} %collective-permute-done.1), channel_id=1, source_target_pairs={{0,4},{4,8},{8,12},{12,16},{16,20},{20,24},{24,28},{28,0},{1,5},{5... | collective-permute-start | bytes 1966088 | tf_op jit(solution)/shard_map/ppermute | solution.py:52
  914.8 16.1 %collective-permute-start.3 = (f32[1280,128]{0,1:T(8,128)S(1)}, f32[1280,128]{0,1:T(8,128)S(1)}, u32[]{:S(2)}, u32[]{:S(2)}) collective-permute-start(f32[1280,128]{0,1:T(8,128)S(1)} %collective-permute-done.2), channel_id=1, source_target_pairs={{0,4},{4,8},{8,12},{12,16},{16,20},{20,24},{24,28},{28,0},{1,5},{5... | collective-permute-start | bytes 1966088 | tf_op jit(solution)/shard_map/ppermute | solution.py:52
  930.9 0.9 copy-start.5
  931.8 15.3 %collective-permute-start.4 = (f32[1280,128]{0,1:T(8,128)S(1)}, f32[1280,128]{0,1:T(8,128)S(1)}, u32[]{:S(2)}, u32[]{:S(2)}) collective-permute-start(f32[1280,128]{0,1:T(8,128)S(1)} %collective-permute-done.3), channel_id=1, source_target_pairs={{0,4},{4,8},{8,12},{12,16},{16,20},{20,24},{24,28},{28,0},{1,5},{5... | collective-permute-start | bytes 1966088 | tf_op jit(solution)/shard_map/ppermute | solution.py:52
  947.1 0.8 copy-start.7
  947.9 14.7 %collective-permute-start.5 = (f32[1280,128]{0,1:T(8,128)S(1)}, f32[1280,128]{0,1:T(8,128)}, u32[]{:S(2)}, u32[]{:S(2)}) collective-permute-start(f32[1280,128]{0,1:T(8,128)S(1)} %collective-permute-done.4), channel_id=1, source_target_pairs={{0,4},{4,8},{8,12},{12,16},{16,20},{20,24},{24,28},{28,0},{1,5},{5... | collective-permute-start | bytes 1966088 | tf_op jit(solution)/shard_map/ppermute | solution.py:52
  962.6 13.9 %collective-permute-start.6 = (f32[1280,128]{0,1:T(8,128)}, f32[1280,128]{0,1:T(8,128)}, u32[]{:S(2)}, u32[]{:S(2)}) collective-permute-start(f32[1280,128]{0,1:T(8,128)} %collective-permute-done.5), channel_id=1, source_target_pairs={{0,4},{4,8},{8,12},{12,16},{16,20},{20,24},{24,28},{28,0},{1,5},{5... | collective-permute-start | bytes 1966088 | tf_op jit(solution)/shard_map/ppermute | solution.py:52
  962.6 21.1 %copy-start.8 = (f32[1280,128]{0,1:T(8,128)S(1)}, f32[1280,128]{0,1:T(8,128)}, u32[]{:S(2)}) copy-start(f32[1280,128]{0,1:T(8,128)} %copy-done.7) | copy-start | bytes 1966084
  962.6 21.2 %copy-start.6 = (f32[1280,128]{0,1:T(8,128)S(1)}, f32[1280,128]{0,1:T(8,128)}, u32[]{:S(2)}) copy-start(f32[1280,128]{0,1:T(8,128)} %copy-done.5) | copy-start | bytes 1966084
Sparse Core Ops, SparseCore 0:
  43.8 36.0 all-reduce.3
  408.9 31.6 all-reduce.5
  696.0 31.6 all-reduce.7
Sparse Core Ops, SparseCore 1:
  73.1 105.6 reduce-scatter.6
  182.9 102.5 reduce-scatter.4
  287.9 85.2 all-gather.2
  469.7 103.0 reduce-scatter.8
  574.9 85.2 all-gather.4
  756.9 103.0 reduce-scatter.10
